TPU v7x, 32 devices: a whole 2x2x4 slice. The times are simulated.
32 devices in a mesh: dp: 4 (over x, core), ctx: 8 (over z, y).
Axes of the slice: x: 2, y: 2, z: 4, core: 2. Of those that a mesh axis runs over, the one named last changes fastest.
Arguments:
- density: float32 [128, 64, 64], P(('dp', 'ctx')), parts along dimension 0, may hold values from 0.1 to 50, as said below
- stem_weight: bfloat16 [216, 1024], replicated, may hold values from -0.4375 to 0.4375
- stem_bias: float32 [1024], replicated, may hold values from -3 to 3
- pos_embed: bfloat16 [2048, 1024], P('ctx'), may hold values from -3 to 3
- ln1_gain: float32 [1024], replicated, may hold values from 0.25 to 1.75
- ln1_bias: float32 [1024], replicated, may hold values from -2 to 2
- w_qkv: bfloat16 [1024, 3072], replicated, may hold values from -2 to 2
- qkv_bias: float32 [3072], replicated, may hold values from -2 to 2
- w_out: bfloat16 [1024, 1024], replicated, may hold values from -0.1875 to 0.1875
- out_bias: float32 [1024], replicated, may hold values from -2 to 2
- ln2_gain: float32 [1024], replicated, may hold values from 0.25 to 1.75
- ln2_bias: float32 [1024], replicated, may hold values from -2 to 2
- w_fc1: bfloat16 [1024, 4096], replicated, may hold values from -0.1875 to 0.1875
- fc1_bias: float32 [4096], replicated, may hold values from -3 to 3
- w_fc2: bfloat16 [4096, 1024], replicated, may hold values from -0.09375 to 0.09375
- fc2_bias: float32 [1024], replicated, may hold values from -2 to 2
Outputs:
- encoded: bfloat16 [8192, 1024], P(('dp', 'ctx')), parts along dimension 0
There are 4 independent parts, one for each index of `dp`. A program takes and returns all parts, laid end to end along the dimension named above; an argument that names none is the same for every part. Nothing has to cross between parts.
Inputs may be any that keep to these rules, and one draw needn't show every extreme that they name: density is positive.
All inputs are finite; a program needn't handle non-finite values.
Results may differ from a plain program's by a relative error of at most 0.013.
Values may be sent and summed in bfloat16 or wider, within the bound.
A program may use at most 384 MiB of HBM per device.

v0:
```python
import functools
import math

import jax
import jax.numpy as jnp
from jax import lax
from jax.experimental import pallas as pl
from jax.experimental.pallas import tpu as pltpu
from jax.sharding import PartitionSpec as P

HEADS = 16
KERNEL = 6
STRIDE = 4
ROWS = 128
MESH = pl.DeviceIdType.MESH
F32 = jnp.float32
BF16 = jnp.bfloat16


def iota(shape, axis):
    return lax.broadcasted_iota(jnp.int32, shape, axis)


def partner(me, mask, n):
    result, bit = 0, 1
    while bit < n:
        result += ((me // bit + mask // bit) % 2) * bit
        bit *= 2
    return result


def norm_rows(values, gain_vector, shift_vector):
    center = values - jnp.mean(values, axis=-1, keepdims=True)
    spread = jnp.mean(center * center, axis=-1, keepdims=True)
    return center * lax.rsqrt(spread + 1e-06) * gain_vector + shift_vector


def layer_kernel(
    n,
    cells,
    density,
    stem_weight,
    stem_bias,
    pos_embed,
    ln1_gain,
    ln1_bias,
    w_qkv_hbm,
    qkv_bias,
    w_out_hbm,
    out_bias,
    ln2_gain,
    ln2_bias,
    w_fc1_hbm,
    fc1_bias,
    w_fc2_hbm,
    fc2_bias,
    encoded,
    w_qkv,
    w_out,
    w_fc1,
    w_fc2,
    weight_sem,
    halo,
    sum_send,
    sum_got,
    edge_send_sem,
    edge_recv_sem,
    sum_send_sem,
    sum_recv_sem,
    select_rows,
    fold,
    planes_wide,
    kernel_rows,
    residual,
    normed,
    outgoing,
    query_got,
    key_got,
    value_got,
    value_wide,
    mixed_send,
    mixed_got,
    attended,
    total,
    send_sem,
    recv_sem,
):
    me = lax.axis_index("ctx")
    planes, side, _ = density.shape
    tokens, width = residual.shape
    head_size = width // HEADS
    local_heads = max(HEADS // n, 1)
    groups = max(n // HEADS, 1)
    group_width = local_heads * head_size
    share = tokens // groups
    grid = side // STRIDE
    window = planes + 2

    weights = [
        pltpu.make_async_copy(source, target, weight_sem.at[i])
        for i, (source, target) in enumerate(
            ((w_qkv_hbm, w_qkv), (w_out_hbm, w_out), (w_fc1_hbm, w_fc1), (w_fc2_hbm, w_fc2))
        )
    ]
    for copy in weights:
        copy.start()

    barrier = pltpu.get_barrier_semaphore()

    def each_peer(action):
        def step(offset, carry):
            action(partner(me, n - offset, n))
            return carry

        lax.fori_loop(1, n, step, 0)

    each_peer(
        lambda peer: pl.semaphore_signal(
            barrier, inc=1, device_id={"ctx": peer}, device_id_type=MESH
        )
    )

    own = jnp.sum(density[...], axis=0)
    own = jnp.sum(own, axis=(0, 1), keepdims=True)
    sum_send[...] = jnp.broadcast_to(own, sum_send.shape)
    sum_got[me] = jnp.broadcast_to(own, sum_send.shape)

    @pl.when(me == 0)
    def _():
        halo[0] = jnp.ones((side, side), F32)

    @pl.when(me == n - 1)
    def _():
        halo[1] = jnp.ones((side, side), F32)

    pl.semaphore_wait(barrier, n - 1)

    def edge(side_index, plane, peer):
        return pltpu.make_async_remote_copy(
            src_ref=density.at[plane],
            dst_ref=halo.at[side_index],
            send_sem=edge_send_sem.at[side_index],
            recv_sem=edge_recv_sem.at[side_index],
            device_id={"ctx": peer},
            device_id_type=MESH,
        )

    up = edge(0, planes - 1, lax.rem(me + 1, n))
    down = edge(1, 0, lax.rem(me + n - 1, n))

    def sum_copy(source, peer):
        return pltpu.make_async_remote_copy(
            src_ref=sum_send,
            dst_ref=sum_got.at[source],
            send_sem=sum_send_sem.at[peer],
            recv_sem=sum_recv_sem.at[source],
            device_id={"ctx": peer},
            device_id_type=MESH,
        )

    each_peer(lambda peer: sum_copy(me, peer).start())

    @pl.when(me < n - 1)
    def _():
        up.start()

    @pl.when(me > 0)
    def _():
        down.start()

    pair = 2 * side
    row = iota((tokens, side), 0)
    col = iota((tokens, side), 1)
    for b in range(KERNEL):
        hit = col == STRIDE * (row // grid) - 1 + b
        select_rows[b] = jnp.where(hit, 1.0, 0.0).astype(BF16)
    lane_row = iota((pair, 256), 0)
    lane_col = iota((pair, 256), 1)
    high = lane_row // side
    offset_c = ((lane_row + 1) & (STRIDE - 1)) + STRIDE * high
    for b in range(KERNEL):
        for a in range(window):
            hit = (offset_c < KERNEL) & (lane_col == (a * KERNEL + b) * KERNEL + offset_c)
            fold[b, a * pair : (a + 1) * pair, :] = jnp.where(hit, 1.0, 0.0).astype(BF16)
    taps = stem_weight.shape[0]
    kernel_rows[...] = jnp.zeros(kernel_rows.shape, BF16)
    kernel_rows[0:taps, :] = stem_weight[...]
    tile_row = iota((tokens, pair), 0)
    tile_lane = iota((tokens, pair), 1)
    keep = (((tile_lane & (side - 1)) + 1) // STRIDE - tile_lane // side) == (
        tile_row & (grid - 1)
    )
    keep = jnp.where(keep, 1.0, 0.0).astype(BF16)

    each_peer(lambda peer: sum_copy(peer, peer).wait_recv())

    @pl.when(me > 0)
    def _():
        up.wait_recv()

    @pl.when(me < n - 1)
    def _():
        down.wait_recv()

    mean_density = (jnp.sum(sum_got[...], axis=0)[0:1, 0:1]) / cells
    for a in range(window):
        if a == 0:
            plane = jnp.where(me > 0, jnp.log(halo[0] / mean_density), 0.0)
        elif a == window - 1:
            plane = jnp.where(me < n - 1, jnp.log(halo[1] / mean_density), 0.0)
        else:
            plane = jnp.log(density[a - 1] / mean_density)
        plane = plane.astype(BF16)
        planes_wide[:, a * pair : (a + 1) * pair] = jnp.concatenate([plane, plane], axis=1)

    keep_wide = jnp.concatenate([keep] * window, axis=1)
    patches = jnp.zeros((tokens, 256), F32)
    for b in range(KERNEL):
        rows = jnp.dot(select_rows[b], planes_wide[...], preferred_element_type=F32)
        rows = rows.astype(BF16) * keep_wide
        patches += jnp.dot(rows, fold[b], preferred_element_type=F32)
    embedded = jnp.dot(patches.astype(BF16), kernel_rows[...], preferred_element_type=F32)
    embedded = embedded + stem_bias[...] + pos_embed[...].astype(F32)
    residual[...] = embedded.astype(BF16)
    normed[...] = norm_rows(residual[...].astype(F32), ln1_gain[...], ln1_bias[...]).astype(BF16)

    def head_group(peer):
        return peer // groups

    def my_rows(peer):
        return pl.ds(pl.multiple_of(lax.rem(peer, groups) * share, share), share)

    def projected_copy(kind, source, peer):
        piece = outgoing.at[kind, head_group(peer)]
        got = (query_got, key_got, value_got)[kind]
        if kind == 0:
            piece = piece.at[my_rows(peer)]
        return pltpu.make_async_remote_copy(
            src_ref=piece,
            dst_ref=got.at[source],
            send_sem=send_sem.at[kind, peer],
            recv_sem=recv_sem.at[kind, source],
            device_id={"ctx": peer},
            device_id_type=MESH,
        )

    weights[0].wait()
    block = 256
    for kind in (1, 2, 0):
        for start in range(0, width, block):
            columns = slice(kind * width + start, kind * width + start + block)
            result = jnp.dot(normed[...], w_qkv[:, columns], preferred_element_type=F32)
            result = result + qkv_bias[:, columns]
            if kind == 0:
                result = result * (1.0 / head_size**0.5)
            result = result.astype(BF16)
            for part in range(block // group_width):
                outgoing[kind, start // group_width + part] = result[
                    :, part * group_width : (part + 1) * group_width
                ]
        each_peer(lambda peer: projected_copy(kind, me, peer).start())
    query_got[me] = outgoing[0, head_group(me), my_rows(me), :]
    key_got[me] = outgoing[1, head_group(me)]
    value_got[me] = outgoing[2, head_group(me)]

    each_peer(lambda peer: projected_copy(1, peer, peer).wait_recv())
    each_peer(lambda peer: projected_copy(2, peer, peer).wait_recv())

    keys_total = n * tokens
    wide = group_width % 128 == 0
    if wide:
        value_wide[:, 0:group_width] = value_got[...].reshape(keys_total, group_width)
        value_wide[:, group_width:] = jnp.ones((keys_total, group_width), BF16)

    def mixed_copy(source, peer):
        return pltpu.make_async_remote_copy(
            src_ref=mixed_send.at[peer],
            dst_ref=mixed_got.at[source],
            send_sem=send_sem.at[3, peer],
            recv_sem=recv_sem.at[3, source],
            device_id={"ctx": peer},
            device_id_type=MESH,
        )

    def attend(offset, carry):
        peer = partner(me, lax.rem(n - offset, n), n)

        @pl.when(offset > 0)
        def _():
            projected_copy(0, peer, peer).wait_recv()

        rows = min(share, ROWS)
        for first in range(0, share, rows):
            query = query_got[peer, first : first + rows, :]
            lane = iota((rows, group_width), 1) // head_size
            mixed = None
            for head in range(local_heads):
                mine = query
                if local_heads > 1:
                    mine = jnp.where(lane == head, query, jnp.zeros_like(query))
                scores = lax.dot_general(
                    mine,
                    key_got[...].reshape(keys_total, group_width),
                    (((1,), (1,)), ((), ())),
                    preferred_element_type=F32,
                )
                weight = jnp.exp(scores - jnp.max(scores, axis=1, keepdims=True))
                values = value_wide[...] if wide else value_got[...].reshape(keys_total, group_width)
                product = jnp.dot(weight.astype(BF16), values, preferred_element_type=F32)
                if wide:
                    part = product[:, 0:group_width] / product[:, group_width:]
                else:
                    part = product / jnp.sum(weight, axis=1, keepdims=True)
                mixed = part if mixed is None else jnp.where(lane == head, part, mixed)
            mixed_send[peer, first : first + rows, :] = mixed.astype(BF16)

        @pl.when(offset > 0)
        def _():
            mixed_copy(me, peer).start()

        @pl.when(offset == 0)
        def _():
            mixed_got[me] = mixed_send[me]

        return carry

    lax.fori_loop(0, n, attend, 0)

    each_peer(lambda peer: mixed_copy(peer, peer).wait_recv())
    for piece in range(n):
        first = (piece % groups) * share
        column = (piece // groups) * group_width
        attended[first : first + share, column : column + group_width] = mixed_got[piece]

    weights[1].wait()
    stream = (
        residual[...].astype(F32)
        + jnp.dot(attended[...], w_out[...], preferred_element_type=F32)
        + out_bias[...]
    ).astype(BF16)
    residual[...] = stream
    stream = stream.astype(F32)
    normed[...] = norm_rows(stream, ln2_gain[...], ln2_bias[...]).astype(BF16)
    total[...] = stream + fc2_bias[...]

    weights[2].wait()
    weights[3].wait()
    hidden_width = w_fc1.shape[1]
    tile = math.gcd(hidden_width, 512)
    for start in range(0, hidden_width, tile):
        columns = slice(start, start + tile)
        hidden = jnp.dot(normed[...], w_fc1[:, columns], preferred_element_type=F32)
        hidden = hidden + fc1_bias[:, columns]
        hidden = 0.5 * hidden * (1.0 + lax.erf(hidden * math.sqrt(0.5)))
        total[...] += jnp.dot(hidden.astype(BF16), w_fc2[columns, :], preferred_element_type=F32)
    encoded[...] = total[...].astype(BF16)

    def finish(peer):
        sum_copy(me, peer).wait_send()
        for kind in range(3):
            projected_copy(kind, me, peer).wait_send()
        mixed_copy(me, peer).wait_send()

    each_peer(finish)

    @pl.when(me < n - 1)
    def _():
        up.wait_send()

    @pl.when(me > 0)
    def _():
        down.wait_send()


def per_device(
    density,
    stem_weight,
    stem_bias,
    pos_embed,
    ln1_gain,
    ln1_bias,
    w_qkv,
    qkv_bias,
    w_out,
    out_bias,
    ln2_gain,
    ln2_bias,
    w_fc1,
    fc1_bias,
    w_fc2,
    fc2_bias,
):
    n = lax.axis_size("ctx")
    tokens, width = pos_embed.shape
    hidden_width = w_fc1.shape[1]
    planes, side, _ = density.shape
    assert planes == STRIDE and tokens == (side // STRIDE) ** 2
    head_size = width // HEADS
    local_heads = max(HEADS // n, 1)
    groups = max(n // HEADS, 1)
    head_groups = HEADS // local_heads
    group_width = local_heads * head_size
    share = tokens // groups
    pair = 2 * side
    window = planes + 2
    vmem = pl.BlockSpec(memory_space=pltpu.VMEM)
    hbm = pl.BlockSpec(memory_space=pl.ANY)

    def line(vector):
        return vector.reshape(1, -1)

    dma = pltpu.SemaphoreType.DMA
    wide_shape = (n * tokens, 2 * group_width) if group_width % 128 == 0 else (16, 128)
    return pl.pallas_call(
        functools.partial(layer_kernel, n, density.size * n),
        out_shape=jax.ShapeDtypeStruct((tokens, width), BF16),
        in_specs=[
            vmem, vmem, vmem, vmem, vmem, vmem, hbm, vmem,
            hbm, vmem, vmem, vmem, hbm, vmem, hbm, vmem,
        ],
        out_specs=vmem,
        scratch_shapes=[
            pltpu.VMEM(w_qkv.shape, BF16),
            pltpu.VMEM(w_out.shape, BF16),
            pltpu.VMEM(w_fc1.shape, BF16),
            pltpu.VMEM(w_fc2.shape, BF16),
            dma((4,)),
            pltpu.VMEM((2, side, side), F32),
            pltpu.VMEM((8, 128), F32),
            pltpu.VMEM((n, 8, 128), F32),
            dma((2,)),
            dma((2,)),
            dma((n,)),
            dma((n,)),
            pltpu.VMEM((KERNEL, tokens, side), BF16),
            pltpu.VMEM((KERNEL, window * pair, 256), BF16),
            pltpu.VMEM((side, window * pair), BF16),
            pltpu.VMEM((256, width), BF16),
            pltpu.VMEM((tokens, width), BF16),
            pltpu.VMEM((tokens, width), BF16),
            pltpu.VMEM((3, head_groups, tokens, group_width), BF16),
            pltpu.VMEM((n, share, group_width), BF16),
            pltpu.VMEM((n, tokens, group_width), BF16),
            pltpu.VMEM((n, tokens, group_width), BF16),
            pltpu.VMEM(wide_shape, BF16),
            pltpu.VMEM((n, share, group_width), BF16),
            pltpu.VMEM((n, share, group_width), BF16),
            pltpu.VMEM((tokens, width), BF16),
            pltpu.VMEM((tokens, width), F32),
            dma((4, n)),
            dma((4, n)),
        ],
        compiler_params=pltpu.CompilerParams(
            collective_id=0, has_side_effects=True, vmem_limit_bytes=60 * 1024 * 1024
        ),
    )(
        density,
        stem_weight,
        line(stem_bias),
        pos_embed,
        line(ln1_gain),
        line(ln1_bias),
        w_qkv,
        line(qkv_bias),
        w_out,
        line(out_bias),
        line(ln2_gain),
        line(ln2_bias),
        w_fc1,
        line(fc1_bias),
        w_fc2,
        line(fc2_bias),
    )


def solution(mesh):
    in_specs = (P(("dp", "ctx"), None, None), P(), P(), P("ctx", None)) + (P(),) * 12
    return jax.shard_map(
        per_device,
        mesh=mesh,
        in_specs=in_specs,
        out_specs=P(("dp", "ctx"), None),
        check_vma=False,
    )
```

profile of v0, /device:TPU:0, one launch (start us, length us, event | category | flops | bytes accessed | tf_op | source)
XLA Modules:
  0.0 72.2 jit_solution(5199820490417347258)
XLA Ops:
  0.0 70.4 %shard_map.154 = bf16[256,1024]{1,0:T(8,128)(2,1)} custom-call(f32[4,64,64]{2,1,0:T(8,128)} %density.1, bf16[216,1024]{1,0:T(8,128)(2,1)} %stem_weight.1, f32[1,1024]{1,0:T(1,128)} %bitcast.11, bf16[256,1024]{1,0:T(8,128)(2,1)} %pos_embed.1, f32[1,1024]{1,0:T(1,128)} %bitcast.12, f32[1,1024]{1,0:T(1,128)} %bitcast.13, bf16[1024,3072]{1,0:T(8,128)(2,1)} %w_qkv_hbm.1, ...), custom_call_target="tpu_custom_call" | custom-call | tf_op jit(solution)/shard_map/pallas_call | solution.py:414
  70.4 1.9 %copy.18 = bf16[256,1024]{1,0:T(8,128)(2,1)} copy(bf16[256,1024]{1,0:T(8,128)(2,1)} %shard_map.154) | data formatting | bytes 1048576
where the time goes:
time: 72.4 us; the launch traced here: 72.2 us
  Pallas kernels  70.4 us (97%)
  local copies, waits for them, and re-layouts  1.87 us (3%)
    pallas_call x1, Pallas kernels, per_device(): pl.pallas_call(functools.partial(layer_kernel, n, density.size * n), out_...  70.4 us
    unnamed x1, local copies, waits for them, and re-layouts  1.87 us

commit v1 on v0

--- a/solution.py
+++ b/solution.py
@@ -3,6 +3,7 @@
 
 import jax
 import jax.numpy as jnp
+import numpy as np
 from jax import lax
 from jax.experimental import pallas as pl
 from jax.experimental.pallas import tpu as pltpu
@@ -372,6 +373,640 @@
         down.wait_send()
 
 
+def stem_tables(side, features):
+    grid = side // STRIDE
+    tokens = grid * grid
+    token = np.arange(tokens)
+    select = np.zeros((STRIDE, tokens, side), np.float32)
+    for b in range(STRIDE):
+        select[b, token, STRIDE * (token // grid) + b] = 1
+    x = np.arange(side)
+    keep = np.tile(x[None, :] // STRIDE == token[:, None] % grid, (1, STRIDE))
+    fold = np.zeros((STRIDE, STRIDE, side, 256), np.float32)
+    for b in range(STRIDE):
+        for a in range(STRIDE):
+            lane = (a * STRIDE + b) * STRIDE + x % STRIDE
+            fold[b, a, x, lane] = 1
+            fold[b, a, x, 192 + lane] = 1
+    expand = np.zeros((3, 3, 128, 256), np.float32)
+    shifts = {0: 0, -1: 1, 1: 2}
+    for a in range(KERNEL):
+        for b in range(KERNEL):
+            for c in range(KERNEL):
+                block = ((a - 1) % STRIDE * STRIDE + (b - 1) % STRIDE) * STRIDE + (c - 1) % STRIDE
+                lane = (a * KERNEL + b) * KERNEL + c
+                expand[shifts[(b - 1) // STRIDE], shifts[(c - 1) // STRIDE], block, lane] = 1
+    return [
+        jnp.asarray(table.reshape(-1, table.shape[-1]), BF16)
+        for table in (select, keep.astype(np.float32), fold, expand)
+    ]
+
+
+def shares_positions(n, replicas, density, pos_embed):
+    planes, side, _ = density.shape
+    tokens, width = pos_embed.shape
+    return (
+        replicas == 4
+        and n % 2 == 0
+        and n <= HEADS
+        and (HEADS // n) * (width // HEADS) == 128
+        and planes == STRIDE
+        and side == 64
+        and tokens == (side // STRIDE) ** 2
+    )
+
+
+def shared_kernel(
+    n,
+    cells,
+    density,
+    stem_weight,
+    stem_bias,
+    pos_embed,
+    ln1_gain,
+    ln1_bias,
+    w_qkv_hbm,
+    qkv_bias,
+    w_out_hbm,
+    out_bias,
+    ln2_gain,
+    ln2_bias,
+    w_fc1_hbm,
+    fc1_bias,
+    w_fc2_hbm,
+    fc2_bias,
+    select_hbm,
+    keep_hbm,
+    fold_hbm,
+    expand_hbm,
+    encoded,
+    w_qkv,
+    w_out,
+    w_fc1,
+    w_fc2,
+    select,
+    keep,
+    fold,
+    expand,
+    qkv_sem,
+    weight_sem,
+    table_sem,
+    sum_send,
+    sum_got,
+    stats_send,
+    stats_got,
+    blocks_send,
+    blocks,
+    windows,
+    kernel_raw,
+    kernel_mixed,
+    position,
+    residual,
+    normed,
+    part_send,
+    part,
+    query,
+    key,
+    value_wide,
+    mixed_send,
+    mixed_got,
+    attended,
+    total,
+    sum_send_sem,
+    sum_recv_sem,
+    stats_send_sem,
+    stats_recv_sem,
+    blocks_send_sem,
+    blocks_recv_sem,
+    part_send_sem,
+    part_recv_sem,
+    mixed_send_sem,
+    mixed_recv_sem,
+):
+    me = lax.axis_index("ctx")
+    replica = lax.axis_index("dp")
+    near = replica + 1 - 2 * lax.rem(replica, 2)
+    across = lax.rem(replica + 2, 4)
+    diagonal = lax.rem(near + 2, 4)
+    tokens, width = residual.shape
+    side = density.shape[1]
+    grid = side // STRIDE
+    head_size = width // HEADS
+    local_heads = HEADS // n
+    lanes = 128
+    share = tokens // 4
+    pairs = n // 2
+    my_pair, my_side = me // 2, lax.rem(me, 2)
+    twin = 2 * my_pair + 1 - my_side
+
+    def pair_at(step):
+        return partner(my_pair, pairs - 1 - step, pairs)
+
+    def qkv_copy(step, kind):
+        start = pl.multiple_of(kind * width + pair_at(step) * 2 * lanes, 2 * lanes)
+        return pltpu.make_async_copy(
+            w_qkv_hbm.at[:, pl.ds(start, 2 * lanes)], w_qkv.at[step, kind], qkv_sem.at[step, kind]
+        )
+
+    tables = [
+        pltpu.make_async_copy(source, target, table_sem.at[i])
+        for i, (source, target) in enumerate(
+            ((select_hbm, select), (keep_hbm, keep), (fold_hbm, fold), (expand_hbm, expand))
+        )
+    ]
+    weights = [
+        pltpu.make_async_copy(source, target, weight_sem.at[i])
+        for i, (source, target) in enumerate(
+            ((w_out_hbm, w_out), (w_fc1_hbm, w_fc1), (w_fc2_hbm, w_fc2))
+        )
+    ]
+    for kind in range(3):
+        qkv_copy(0, kind).start()
+    for copy in tables:
+        copy.start()
+    for step in range(1, pairs):
+        for kind in range(3):
+            qkv_copy(step, kind).start()
+
+    barrier = pltpu.get_barrier_semaphore()
+
+    def each_peer(action):
+        def step(offset, carry):
+            action(partner(me, n - offset, n))
+            return carry
+
+        lax.fori_loop(1, n, step, 0)
+
+    each_peer(
+        lambda peer: pl.semaphore_signal(
+            barrier, inc=1, device_id={"ctx": peer}, device_id_type=MESH
+        )
+    )
+    for other in (near, across):
+        pl.semaphore_signal(barrier, inc=1, device_id={"dp": other}, device_id_type=MESH)
+
+    own = jnp.sum(density[...], axis=0)
+    own = jnp.sum(own, axis=(0, 1), keepdims=True)
+    sum_send[...] = jnp.broadcast_to(own, sum_send.shape)
+    sum_got[me] = jnp.broadcast_to(own, sum_send.shape)
+    pl.semaphore_wait(barrier, n + 1)
+
+    def remote(source, target, send, recv, **device):
+        return pltpu.make_async_remote_copy(
+            src_ref=source,
+            dst_ref=target,
+            send_sem=send,
+            recv_sem=recv,
+            device_id=device,
+            device_id_type=MESH,
+        )
+
+    def sum_copy(source, peer):
+        return remote(
+            sum_send, sum_got.at[source], sum_send_sem.at[peer], sum_recv_sem.at[source], ctx=peer
+        )
+
+    each_peer(lambda peer: sum_copy(me, peer).start())
+
+    centred = pos_embed[...].astype(F32) + stem_bias[...]
+    centred = centred - jnp.mean(centred, axis=1, keepdims=True)
+    position[...] = (centred * ln1_gain[...]).astype(BF16)
+
+    def rows_of(which):
+        return pl.ds(pl.multiple_of(which * share, share), share)
+
+    def part_copy(step, other):
+        return remote(
+            part_send.at[2 * step + other],
+            part.at[me, rows_of(replica)],
+            part_send_sem.at[0, 2 * step + other],
+            part_recv_sem.at[0, me],
+            ctx=2 * pair_at(step) + other,
+        )
+
+    def part_got(source):
+        return remote(
+            part_send.at[0],
+            part.at[source, rows_of(replica)],
+            part_send_sem.at[0, 0],
+            part_recv_sem.at[0, source],
+            ctx=source,
+        )
+
+    def relay(hop, source, owner, target):
+        piece = part.at[source, rows_of(owner)]
+        return remote(
+            piece, piece, part_send_sem.at[hop, source], part_recv_sem.at[hop, source], dp=target
+        )
+
+    def project_positions(step):
+        rows = position[rows_of(replica), :]
+        for kind in range(3):
+            qkv_copy(step, kind).wait()
+            result = jnp.dot(rows, w_qkv[step, kind], preferred_element_type=F32).astype(BF16)
+            for other in range(2):
+                part_send[2 * step + other, :, kind * lanes : (kind + 1) * lanes] = result[
+                    :, other * lanes : (other + 1) * lanes
+                ]
+        for other in range(2):
+            if step < pairs - 1:
+                part_copy(step, other).start()
+            else:
+
+                @pl.when(my_side != other)
+                def _():
+                    part_copy(step, other).start()
+
+    project_positions(0)
+
+    each_peer(lambda peer: sum_copy(peer, peer).wait_recv())
+    mean_density = (jnp.sum(sum_got[...], axis=0)[0:1, 0:1]) / cells
+    for copy in tables:
+        copy.wait()
+    planes = [jnp.log(density[a] / mean_density).astype(BF16) for a in range(STRIDE)]
+    planes = jnp.concatenate(planes, axis=1)
+    picked = jnp.dot(select[...], planes, preferred_element_type=F32).astype(BF16)
+    picked = [picked[b * tokens : (b + 1) * tokens] * keep[...] for b in range(STRIDE)]
+    folded = jnp.dot(jnp.concatenate(picked, axis=1), fold[...], preferred_element_type=F32)
+    half = tokens // 2
+    folded = folded[0:half, 0:lanes] + folded[half:, lanes:]
+    blocks_send[...] = folded.astype(BF16)
+    blocks[me] = folded.astype(BF16)
+
+    def blocks_copy(slot, peer):
+        return remote(
+            blocks_send,
+            blocks.at[me],
+            blocks_send_sem.at[slot],
+            blocks_recv_sem.at[me],
+            ctx=peer,
+        )
+
+    def blocks_relay(source, slot):
+        return remote(
+            blocks.at[source],
+            blocks.at[source],
+            blocks_send_sem.at[slot],
+            blocks_recv_sem.at[source],
+            ctx=twin,
+        )
+
+    for step in range(pairs - 1):
+        blocks_copy(step, 2 * pair_at(step) + my_side).start()
+    blocks_copy(pairs - 1, twin).start()
+
+    for step in range(1, pairs):
+        project_positions(step)
+    for copy in weights:
+        copy.start()
+
+    my_lanes = pl.ds(pl.multiple_of(my_side * lanes, lanes), lanes)
+    mine = jnp.concatenate([w_qkv[pairs - 1, kind, :, my_lanes] for kind in range(3)], axis=1)
+    part[me] = jnp.dot(position[...], mine, preferred_element_type=F32).astype(BF16)
+    taps = stem_weight.shape[0]
+    kernel_raw[...] = jnp.zeros(kernel_raw.shape, BF16)
+    kernel_raw[0:taps, :] = stem_weight[...]
+    kernel_mixed[...] = jnp.zeros(kernel_mixed.shape, BF16)
+    kernel = stem_weight[...].astype(F32)
+    kernel = (kernel - jnp.mean(kernel, axis=1, keepdims=True)) * ln1_gain[...]
+    kernel_mixed[0:taps, :] = kernel.astype(BF16)
+    high = ln1_bias[...].astype(BF16)
+    low = (ln1_bias[...] - high.astype(F32)).astype(BF16)
+    line = iota((8, width), 0)
+    bias_rows = jnp.where(line == 0, high.astype(F32), jnp.where(line == 1, low.astype(F32), 0.0))
+    kernel_mixed[taps : taps + 8, :] = bias_rows.astype(BF16)
+    mixing = jnp.dot(kernel_mixed[...], mine, preferred_element_type=F32)
+    shift = mixing[taps : taps + 1] + mixing[taps + 1 : taps + 2]
+    my_bias = [
+        qkv_bias[:, pl.ds(pl.multiple_of(kind * width + me * lanes, lanes), lanes)]
+        for kind in range(3)
+    ]
+    shift = shift + jnp.concatenate(my_bias, axis=1)
+    mixing = mixing.astype(BF16)
+
+    def relay_first(step):
+        for other in range(2):
+
+            def pass_on():
+                source = 2 * pair_at(step) + other
+                part_got(source).wait_recv()
+                relay(1, source, replica, near).start()
+                relay(2, source, replica, across).start()
+
+            if step < pairs - 1:
+                pass_on()
+            else:
+                pl.when(my_side != other)(pass_on)
+
+    def relay_second(step):
+        for other in range(2):
+
+            def pass_on():
+                source = 2 * pair_at(step) + other
+                relay(2, source, across, across).wait_recv()
+                relay(3, source, across, near).start()
+
+            if step < pairs - 1:
+                pass_on()
+            else:
+                pl.when(my_side != other)(pass_on)
+
+    relay_first(0)
+    for step in range(pairs - 1):
+        source = 2 * pair_at(step) + my_side
+        blocks_relay(source, 0).wait_recv()
+        blocks_relay(source, pairs + step).start()
+    relay_first(1)
+    for step in range(pairs):
+        source = 2 * pair_at(step) + 1 - my_side
+        blocks_relay(source, 0).wait_recv()
+
+    for t in range(n):
+        packed = blocks[t].astype(F32)
+        spread = jnp.concatenate([packed, pltpu.roll(packed, lanes // 2, 1)], axis=0)
+        column = iota(spread.shape, 0) & (grid - 1)
+        before = jnp.where(column == 0, 0.0, pltpu.roll(spread, 1, 0))
+        after = jnp.where(column == grid - 1, 0.0, pltpu.roll(spread, tokens - 1, 0))
+        wide = jnp.concatenate([v.astype(BF16) for v in (spread, before, after)], axis=1)
+        edge = jnp.zeros((grid, wide.shape[1]), BF16)
+        above = jnp.concatenate([edge, wide[: tokens - grid]], axis=0)
+        below = jnp.concatenate([wide[grid:], edge], axis=0)
+        wide = jnp.concatenate([wide, above, below], axis=1)
+        windows[t] = jnp.dot(wide, expand[...], preferred_element_type=F32).astype(BF16)
+
+    tap = iota((tokens, 256), 1)
+    face = KERNEL * KERNEL
+
+    def patches_of(before, here, after):
+        inner = jnp.where(tap < taps - face, here, after)
+        return jnp.where(tap < face, before, inner)
+
+    before = windows[lax.rem(me + n - 1, n)]
+    after = windows[lax.rem(me + 1, n)]
+    before = jnp.where(me > 0, before, jnp.zeros_like(before))
+    after = jnp.where(me < n - 1, after, jnp.zeros_like(after))
+    patches = patches_of(before, windows[me], after)
+    embedded = jnp.dot(patches, kernel_raw[...], preferred_element_type=F32)
+    embedded = embedded + stem_bias[...] + pos_embed[...].astype(F32)
+    residual[...] = embedded.astype(BF16)
+    centre = residual[...].astype(F32)
+    centre = centre - jnp.mean(centre, axis=1, keepdims=True)
+    inverse = lax.rsqrt(jnp.mean(centre * centre, axis=1, keepdims=True) + 1e-06)
+    inverse = jnp.broadcast_to(inverse, (tokens, lanes))
+    stats = [inverse[i * lanes : (i + 1) * lanes].T[0:1] for i in range(tokens // lanes)]
+    stats.append(jnp.zeros((8 - len(stats), lanes), F32))
+    stats = jnp.concatenate(stats, axis=0)
+    stats_send[...] = stats
+    stats_got[me] = stats
+
+    def stats_copy(source, peer):
+        return remote(
+            stats_send,
+            stats_got.at[source],
+            stats_send_sem.at[peer],
+            stats_recv_sem.at[source],
+            ctx=peer,
+        )
+
+    each_peer(lambda peer: stats_copy(me, peer).start())
+
+    relay_second(0)
+    for step in range(2, pairs):
+        relay_first(step)
+        relay_second(step - 1)
+    relay_second(pairs - 1)
+
+    each_peer(lambda peer: stats_copy(peer, peer).wait_recv())
+
+    def arrived(source):
+        relay(1, source, near, near).wait_recv()
+        relay(3, source, diagonal, near).wait_recv()
+
+    each_peer(arrived)
+
+    scales = (1.0 / head_size**0.5, 1.0, 1.0)
+    for t in range(n):
+        nothing = jnp.zeros((tokens, 256), BF16)
+        patches = patches_of(
+            windows[t - 1] if t > 0 else nothing,
+            windows[t],
+            windows[t + 1] if t < n - 1 else nothing,
+        )
+        result = jnp.dot(patches, mixing, preferred_element_type=F32) + part[t].astype(F32)
+        inverse = jnp.concatenate(
+            [
+                jnp.broadcast_to(stats_got[t, i : i + 1, :], (lanes, lanes)).T
+                for i in range(tokens // lanes)
+            ],
+            axis=0,
+        )
+        for kind, scale in enumerate(scales):
+            columns = slice(kind * lanes, (kind + 1) * lanes)
+            rows = result[:, columns] * inverse + shift[:, columns]
+            if kind == 0:
+                query[t] = (rows * scale).astype(BF16)
+            elif kind == 1:
+                key[t] = rows.astype(BF16)
+            else:
+                value_wide[t * tokens : (t + 1) * tokens, 0:lanes] = rows.astype(BF16)
+    keys_total = n * tokens
+    value_wide[:, lanes:] = jnp.ones((keys_total, lanes), BF16)
+
+    def mixed_copy(source, peer):
+        return remote(
+            mixed_send.at[peer],
+            mixed_got.at[source],
+            mixed_send_sem.at[peer],
+            mixed_recv_sem.at[source],
+            ctx=peer,
+        )
+
+    def attend(offset, carry):
+        peer = partner(me, n - 1 - offset, n)
+        rows = min(tokens, ROWS)
+        for first in range(0, tokens, rows):
+            picked = query[peer, first : first + rows, :]
+            lane = iota((rows, lanes), 1) // head_size
+            mixed = None
+            for head in range(local_heads):
+                mine = jnp.where(lane == head, picked, jnp.zeros_like(picked))
+                scores = lax.dot_general(
+                    mine,
+                    key[...].reshape(keys_total, lanes),
+                    (((1,), (1,)), ((), ())),
+                    preferred_element_type=F32,
+                )
+                weight = jnp.exp(scores - jnp.max(scores, axis=1, keepdims=True))
+                product = jnp.dot(
+                    weight.astype(BF16), value_wide[...], preferred_element_type=F32
+                )
+                rows_mixed = product[:, 0:lanes] / product[:, lanes:]
+                mixed = rows_mixed if mixed is None else jnp.where(lane == head, rows_mixed, mixed)
+            mixed_send[peer, first : first + rows, :] = mixed.astype(BF16)
+
+        @pl.when(offset < n - 1)
+        def _():
+            mixed_copy(me, peer).start()
+
+        return carry
+
+    lax.fori_loop(0, n, attend, 0)
+    mixed_got[me] = mixed_send[me]
+
+    each_peer(lambda peer: mixed_copy(peer, peer).wait_recv())
+    for piece in range(n):
+        attended[:, piece * lanes : (piece + 1) * lanes] = mixed_got[piece]
+
+    weights[0].wait()
+    stream = (
+        residual[...].astype(F32)
+        + jnp.dot(attended[...], w_out[...], preferred_element_type=F32)
+        + out_bias[...]
+    ).astype(BF16)
+    stream = stream.astype(F32)
+    normed[...] = norm_rows(stream, ln2_gain[...], ln2_bias[...]).astype(BF16)
+    total[...] = stream + fc2_bias[...]
+
+    weights[1].wait()
+    weights[2].wait()
+    hidden_width = w_fc1.shape[1]
+    tile = math.gcd(hidden_width, 512)
+    for start in range(0, hidden_width, tile):
+        columns = slice(start, start + tile)
+        hidden = jnp.dot(normed[...], w_fc1[:, columns], preferred_element_type=F32)
+        hidden = hidden + fc1_bias[:, columns]
+        hidden = 0.5 * hidden * (1.0 + lax.erf(hidden * math.sqrt(0.5)))
+        total[...] += jnp.dot(hidden.astype(BF16), w_fc2[columns, :], preferred_element_type=F32)
+    encoded[...] = total[...].astype(BF16)
+
+    def finish(peer):
+        sum_copy(me, peer).wait_send()
+        stats_copy(me, peer).wait_send()
+        mixed_copy(me, peer).wait_send()
+        relay(1, peer, replica, near).wait_send()
+        relay(2, peer, replica, across).wait_send()
+        relay(3, peer, across, near).wait_send()
+
+    each_peer(finish)
+    for step in range(pairs - 1):
+        for other in range(2):
+            part_copy(step, other).wait_send()
+        blocks_copy(step, 2 * pair_at(step) + my_side).wait_send()
+        blocks_relay(2 * pair_at(step) + my_side, pairs + step).wait_send()
+    for other in range(2):
+
+        @pl.when(my_side != other)
+        def _():
+            part_copy(pairs - 1, other).wait_send()
+
+    blocks_copy(pairs - 1, twin).wait_send()
+
+
+def shared_call(
+    density,
+    stem_weight,
+    stem_bias,
+    pos_embed,
+    ln1_gain,
+    ln1_bias,
+    w_qkv,
+    qkv_bias,
+    w_out,
+    out_bias,
+    ln2_gain,
+    ln2_bias,
+    w_fc1,
+    fc1_bias,
+    w_fc2,
+    fc2_bias,
+):
+    n = lax.axis_size("ctx")
+    tokens, width = pos_embed.shape
+    side = density.shape[1]
+    vmem = pl.BlockSpec(memory_space=pltpu.VMEM)
+    hbm = pl.BlockSpec(memory_space=pl.ANY)
+    tables = stem_tables(side, stem_weight.shape[0])
+
+    def line(vector):
+        return vector.reshape(1, -1)
+
+    dma = pltpu.SemaphoreType.DMA
+    lanes = 128
+    pairs = n // 2
+    return pl.pallas_call(
+        functools.partial(shared_kernel, n, density.size * n),
+        out_shape=jax.ShapeDtypeStruct((tokens, width), BF16),
+        in_specs=[
+            vmem, vmem, vmem, vmem, vmem, vmem, hbm, vmem,
+            hbm, vmem, vmem, vmem, hbm, vmem, hbm, vmem,
+            hbm, hbm, hbm, hbm,
+        ],
+        out_specs=vmem,
+        scratch_shapes=[
+            pltpu.VMEM((pairs, 3, width, 2 * lanes), BF16),
+            pltpu.VMEM(w_out.shape, BF16),
+            pltpu.VMEM(w_fc1.shape, BF16),
+            pltpu.VMEM(w_fc2.shape, BF16),
+            *[pltpu.VMEM(table.shape, BF16) for table in tables],
+            dma((pairs, 3)),
+            dma((3,)),
+            dma((4,)),
+            pltpu.VMEM((8, lanes), F32),
+            pltpu.VMEM((n, 8, lanes), F32),
+            pltpu.VMEM((8, lanes), F32),
+            pltpu.VMEM((n, 8, lanes), F32),
+            pltpu.VMEM((tokens // 2, lanes), BF16),
+            pltpu.VMEM((n, tokens // 2, lanes), BF16),
+            pltpu.VMEM((n, tokens, 256), BF16),
+            pltpu.VMEM((256, width), BF16),
+            pltpu.VMEM((256, width), BF16),
+            pltpu.VMEM((tokens, width), BF16),
+            pltpu.VMEM((tokens, width), BF16),
+            pltpu.VMEM((tokens, width), BF16),
+            pltpu.VMEM((n, tokens // 4, 3 * lanes), BF16),
+            pltpu.VMEM((n, tokens, 3 * lanes), BF16),
+            pltpu.VMEM((n, tokens, lanes), BF16),
+            pltpu.VMEM((n, tokens, lanes), BF16),
+            pltpu.VMEM((n * tokens, 2 * lanes), BF16),
+            pltpu.VMEM((n, tokens, lanes), BF16),
+            pltpu.VMEM((n, tokens, lanes), BF16),
+            pltpu.VMEM((tokens, width), BF16),
+            pltpu.VMEM((tokens, width), F32),
+            dma((n,)),
+            dma((n,)),
+            dma((n,)),
+            dma((n,)),
+            dma((2 * pairs,)),
+            dma((n,)),
+            dma((4, n)),
+            dma((4, n)),
+            dma((n,)),
+            dma((n,)),
+        ],
+        compiler_params=pltpu.CompilerParams(
+            collective_id=1, has_side_effects=True, vmem_limit_bytes=60 * 1024 * 1024
+        ),
+    )(
+        density,
+        stem_weight,
+        line(stem_bias),
+        pos_embed,
+        line(ln1_gain),
+        line(ln1_bias),
+        w_qkv,
+        line(qkv_bias),
+        w_out,
+        line(out_bias),
+        line(ln2_gain),
+        line(ln2_bias),
+        w_fc1,
+        line(fc1_bias),
+        w_fc2,
+        line(fc2_bias),
+        *tables,
+    )
+
+
 def per_device(
     density,
     stem_weight,
@@ -392,6 +1027,11 @@
 ):
     n = lax.axis_size("ctx")
     tokens, width = pos_embed.shape
+    if shares_positions(n, lax.axis_size("dp"), density, pos_embed):
+        return shared_call(
+            density, stem_weight, stem_bias, pos_embed, ln1_gain, ln1_bias, w_qkv, qkv_bias,
+            w_out, out_bias, ln2_gain, ln2_bias, w_fc1, fc1_bias, w_fc2, fc2_bias,
+        )
     hidden_width = w_fc1.shape[1]
     planes, side, _ = density.shape
     assert planes == STRIDE and tokens == (side // STRIDE) ** 2

time: 72.4 us -> 58.8 us (0.81)
  Pallas kernels: 70.4 us -> 56.7 us
    pallas_call x1, Pallas kernels: 70.4 us -> 56.7 us  [shared_call(): pl.pallas_call(functools.partial(shared_kernel, n, density.size * n), out...]
where the time goes in v1:
time: 58.8 us; the launch traced here: 58.6 us
  Pallas kernels  56.7 us (96%)
  local copies, waits for them, and re-layouts  1.87 us (3%)
    pallas_call x1, Pallas kernels, shared_call(): pl.pallas_call(functools.partial(shared_kernel, n, density.size * n), out...  56.7 us
    unnamed x1, local copies, waits for them, and re-layouts  1.87 us

profile of v1, /device:TPU:0, one launch (start us, length us, event | category | flops | bytes accessed | tf_op | source)
XLA Modules:
  0.0 58.6 jit_solution(8850372175074786699)
XLA Ops:
  0.0 56.7 %shard_map.190 = bf16[256,1024]{1,0:T(8,128)(2,1)} custom-call(f32[4,64,64]{2,1,0:T(8,128)} %density.1, bf16[216,1024]{1,0:T(8,128)(2,1)} %stem_weight.1, f32[1,1024]{1,0:T(1,128)} %bitcast.11, bf16[256,1024]{1,0:T(8,128)(2,1)} %pos_embed.1, f32[1,1024]{1,0:T(1,128)} %bitcast.12, f32[1,1024]{1,0:T(1,128)} %bitcast.13, bf16[1024,3072]{1,0:T(8,128)(2,1)} %w_qkv_hbm.1, ...), custom_call_target="tpu_custom_call" | custom-call | tf_op jit(solution)/shard_map/pallas_call | solution.py:936
  56.7 1.9 %copy.22 = bf16[256,1024]{1,0:T(8,128)(2,1)} copy(bf16[256,1024]{1,0:T(8,128)(2,1)} %shard_map.190) | data formatting | bytes 1048576

commit v2 on v1

--- a/solution.py
+++ b/solution.py
@@ -470,7 +470,6 @@
     value_wide,
     mixed_send,
     mixed_got,
-    attended,
     total,
     sum_send_sem,
     sum_recv_sem,
@@ -502,11 +501,11 @@
     def pair_at(step):
         return partner(my_pair, pairs - 1 - step, pairs)
 
-    def qkv_copy(step, kind):
-        start = pl.multiple_of(kind * width + pair_at(step) * 2 * lanes, 2 * lanes)
-        return pltpu.make_async_copy(
-            w_qkv_hbm.at[:, pl.ds(start, 2 * lanes)], w_qkv.at[step, kind], qkv_sem.at[step, kind]
-        )
+    depth = width // 4
+
+    def qkv_copy(piece):
+        rows = pl.ds(piece * depth, depth)
+        return pltpu.make_async_copy(w_qkv_hbm.at[rows], w_qkv.at[rows], qkv_sem.at[piece])
 
     tables = [
         pltpu.make_async_copy(source, target, table_sem.at[i])
@@ -520,13 +519,10 @@
             ((w_out_hbm, w_out), (w_fc1_hbm, w_fc1), (w_fc2_hbm, w_fc2))
         )
     ]
-    for kind in range(3):
-        qkv_copy(0, kind).start()
     for copy in tables:
         copy.start()
-    for step in range(1, pairs):
-        for kind in range(3):
-            qkv_copy(step, kind).start()
+    for piece in range(4):
+        qkv_copy(piece).start()
 
     barrier = pltpu.get_barrier_semaphore()
 
@@ -545,12 +541,15 @@
     for other in (near, across):
         pl.semaphore_signal(barrier, inc=1, device_id={"dp": other}, device_id_type=MESH)
 
-    own = jnp.sum(density[...], axis=0)
-    own = jnp.sum(own, axis=(0, 1), keepdims=True)
-    sum_send[...] = jnp.broadcast_to(own, sum_send.shape)
-    sum_got[me] = jnp.broadcast_to(own, sum_send.shape)
-    pl.semaphore_wait(barrier, n + 1)
-
+    def everywhere(values):
+        return jnp.sum(jnp.sum(values, axis=0), axis=(0, 1), keepdims=True)
+
+    logs = jnp.log(density[...])
+    level = everywhere(logs) / (density.shape[0] * side * side)
+    line = iota(sum_send.shape, 0)
+    own = jnp.where(line == 0, everywhere(density[...]), level)
+    sum_send[...] = own
+    sum_got[me] = own
     def remote(source, target, send, recv, **device):
         return pltpu.make_async_remote_copy(
             src_ref=source,
@@ -566,7 +565,6 @@
             sum_send, sum_got.at[source], sum_send_sem.at[peer], sum_recv_sem.at[source], ctx=peer
         )
 
-    each_peer(lambda peer: sum_copy(me, peer).start())
 
     centred = pos_embed[...].astype(F32) + stem_bias[...]
     centred = centred - jnp.mean(centred, axis=1, keepdims=True)
@@ -575,22 +573,13 @@
     def rows_of(which):
         return pl.ds(pl.multiple_of(which * share, share), share)
 
-    def part_copy(step, other):
+    def part_copy(source, peer):
         return remote(
-            part_send.at[2 * step + other],
-            part.at[me, rows_of(replica)],
-            part_send_sem.at[0, 2 * step + other],
-            part_recv_sem.at[0, me],
-            ctx=2 * pair_at(step) + other,
-        )
-
-    def part_got(source):
-        return remote(
-            part_send.at[0],
+            part_send.at[peer],
             part.at[source, rows_of(replica)],
-            part_send_sem.at[0, 0],
+            part_send_sem.at[0, peer],
             part_recv_sem.at[0, source],
-            ctx=source,
+            ctx=peer,
         )
 
     def relay(hop, source, owner, target):
@@ -599,32 +588,9 @@
             piece, piece, part_send_sem.at[hop, source], part_recv_sem.at[hop, source], dp=target
         )
 
-    def project_positions(step):
-        rows = position[rows_of(replica), :]
-        for kind in range(3):
-            qkv_copy(step, kind).wait()
-            result = jnp.dot(rows, w_qkv[step, kind], preferred_element_type=F32).astype(BF16)
-            for other in range(2):
-                part_send[2 * step + other, :, kind * lanes : (kind + 1) * lanes] = result[
-                    :, other * lanes : (other + 1) * lanes
-                ]
-        for other in range(2):
-            if step < pairs - 1:
-                part_copy(step, other).start()
-            else:
-
-                @pl.when(my_side != other)
-                def _():
-                    part_copy(step, other).start()
-
-    project_positions(0)
-
-    each_peer(lambda peer: sum_copy(peer, peer).wait_recv())
-    mean_density = (jnp.sum(sum_got[...], axis=0)[0:1, 0:1]) / cells
     for copy in tables:
         copy.wait()
-    planes = [jnp.log(density[a] / mean_density).astype(BF16) for a in range(STRIDE)]
-    planes = jnp.concatenate(planes, axis=1)
+    planes = jnp.concatenate([(logs[a] - level).astype(BF16) for a in range(STRIDE)], axis=1)
     picked = jnp.dot(select[...], planes, preferred_element_type=F32).astype(BF16)
     picked = [picked[b * tokens : (b + 1) * tokens] * keep[...] for b in range(STRIDE)]
     folded = jnp.dot(jnp.concatenate(picked, axis=1), fold[...], preferred_element_type=F32)
@@ -651,17 +617,39 @@
             ctx=twin,
         )
 
+    pl.semaphore_wait(barrier, n + 1)
+    each_peer(lambda peer: sum_copy(me, peer).start())
+    corner = me - 1 + 2 * my_side
+    inside = (1 - my_side) * ((me + n - 1) // n) + my_side * ((2 * n - 2 - me) // n)
+
+    @pl.when(inside == 1)
+    def _():
+        blocks_copy(pairs, corner).start()
+
+    blocks_copy(pairs - 1, twin).start()
     for step in range(pairs - 1):
         blocks_copy(step, 2 * pair_at(step) + my_side).start()
-    blocks_copy(pairs - 1, twin).start()
-
-    for step in range(1, pairs):
-        project_positions(step)
+
+    for piece in range(4):
+        qkv_copy(piece).wait()
+    rows = position[rows_of(replica), :]
+    for kind in range(3):
+        result = jnp.dot(
+            rows, w_qkv[:, kind * width : (kind + 1) * width], preferred_element_type=F32
+        ).astype(BF16)
+        for peer in range(n):
+            part_send[peer, :, kind * lanes : (kind + 1) * lanes] = result[
+                :, peer * lanes : (peer + 1) * lanes
+            ]
+    for mask in range(1, n):
+        part_copy(me, partner(me, mask, n)).start()
     for copy in weights:
         copy.start()
 
-    my_lanes = pl.ds(pl.multiple_of(my_side * lanes, lanes), lanes)
-    mine = jnp.concatenate([w_qkv[pairs - 1, kind, :, my_lanes] for kind in range(3)], axis=1)
+    def my_lanes(kind):
+        return pl.ds(pl.multiple_of(kind * width + me * lanes, lanes), lanes)
+
+    mine = jnp.concatenate([w_qkv[:, my_lanes(kind)] for kind in range(3)], axis=1)
     part[me] = jnp.dot(position[...], mine, preferred_element_type=F32).astype(BF16)
     taps = stem_weight.shape[0]
     kernel_raw[...] = jnp.zeros(kernel_raw.shape, BF16)
@@ -677,52 +665,34 @@
     kernel_mixed[taps : taps + 8, :] = bias_rows.astype(BF16)
     mixing = jnp.dot(kernel_mixed[...], mine, preferred_element_type=F32)
     shift = mixing[taps : taps + 1] + mixing[taps + 1 : taps + 2]
-    my_bias = [
-        qkv_bias[:, pl.ds(pl.multiple_of(kind * width + me * lanes, lanes), lanes)]
-        for kind in range(3)
-    ]
+    my_bias = [qkv_bias[:, my_lanes(kind)] for kind in range(3)]
     shift = shift + jnp.concatenate(my_bias, axis=1)
     mixing = mixing.astype(BF16)
 
-    def relay_first(step):
-        for other in range(2):
-
-            def pass_on():
-                source = 2 * pair_at(step) + other
-                part_got(source).wait_recv()
-                relay(1, source, replica, near).start()
-                relay(2, source, replica, across).start()
-
-            if step < pairs - 1:
-                pass_on()
-            else:
-                pl.when(my_side != other)(pass_on)
-
-    def relay_second(step):
-        for other in range(2):
-
-            def pass_on():
-                source = 2 * pair_at(step) + other
-                relay(2, source, across, across).wait_recv()
-                relay(3, source, across, near).start()
-
-            if step < pairs - 1:
-                pass_on()
-            else:
-                pl.when(my_side != other)(pass_on)
-
-    relay_first(0)
-    for step in range(pairs - 1):
-        source = 2 * pair_at(step) + my_side
-        blocks_relay(source, 0).wait_recv()
-        blocks_relay(source, pairs + step).start()
-    relay_first(1)
-    for step in range(pairs):
-        source = 2 * pair_at(step) + 1 - my_side
-        blocks_relay(source, 0).wait_recv()
-
-    for t in range(n):
-        packed = blocks[t].astype(F32)
+    def relay_first(*masks):
+        for mask in masks:
+            source = partner(me, mask, n)
+            part_copy(source, source).wait_recv()
+            relay(1, source, replica, near).start()
+            relay(2, source, replica, across).start()
+
+    def relay_second(*masks):
+        for mask in masks:
+            source = partner(me, mask, n)
+            relay(2, source, across, across).wait_recv()
+            relay(3, source, across, near).start()
+
+    each_peer(lambda peer: sum_copy(peer, peer).wait_recv())
+    blocks_relay(twin, 0).wait_recv()
+
+    @pl.when(inside == 1)
+    def _():
+        blocks_relay(corner, 0).wait_recv()
+
+    log_mean = jnp.log(jnp.sum(sum_got[...], axis=0)[0:1, 0:1] / cells)
+
+    def spread_windows(t):
+        packed = blocks[t].astype(F32) + (sum_got[t][1:2, 0:1] - log_mean)
         spread = jnp.concatenate([packed, pltpu.roll(packed, lanes // 2, 1)], axis=0)
         column = iota(spread.shape, 0) & (grid - 1)
         before = jnp.where(column == 0, 0.0, pltpu.roll(spread, 1, 0))
@@ -734,6 +704,9 @@
         wide = jnp.concatenate([wide, above, below], axis=1)
         windows[t] = jnp.dot(wide, expand[...], preferred_element_type=F32).astype(BF16)
 
+    for t in (me, twin, me + inside * (2 * my_side - 1)):
+        spread_windows(t)
+
     tap = iota((tokens, 256), 1)
     face = KERNEL * KERNEL
 
@@ -741,8 +714,8 @@
         inner = jnp.where(tap < taps - face, here, after)
         return jnp.where(tap < face, before, inner)
 
-    before = windows[lax.rem(me + n - 1, n)]
-    after = windows[lax.rem(me + 1, n)]
+    before = windows[me - (me + n - 1) // n]
+    after = windows[me + (2 * n - 2 - me) // n]
     before = jnp.where(me > 0, before, jnp.zeros_like(before))
     after = jnp.where(me < n - 1, after, jnp.zeros_like(after))
     patches = patches_of(before, windows[me], after)
@@ -770,11 +743,31 @@
 
     each_peer(lambda peer: stats_copy(me, peer).start())
 
-    relay_second(0)
-    for step in range(2, pairs):
-        relay_first(step)
-        relay_second(step - 1)
-    relay_second(pairs - 1)
+    twin_corner = twin + 1 - 2 * my_side
+    for step in range(pairs - 1):
+        source = 2 * pair_at(step) + my_side
+        blocks_relay(source, 0).wait_recv()
+
+        @pl.when(source != twin_corner)
+        def _():
+            blocks_relay(source, pairs + 1 + step).start()
+
+    relay_first(*range(1, n // 2))
+    for step in range(pairs - 1):
+        source = 2 * pair_at(step) + 1 - my_side
+
+        @pl.when(source != corner)
+        def _():
+            blocks_relay(source, 0).wait_recv()
+
+    for mask in range(2, n):
+        spread_windows(partner(me, mask, n))
+    lag = n // 2 - 2
+    for mask in range(1, n + lag):
+        if n // 2 <= mask < n:
+            relay_first(mask)
+        if mask > lag:
+            relay_second(mask - lag)
 
     each_peer(lambda peer: stats_copy(peer, peer).wait_recv())
 
@@ -806,71 +799,80 @@
             if kind == 0:
                 query[t] = (rows * scale).astype(BF16)
             elif kind == 1:
-                key[t] = rows.astype(BF16)
+                key[:, t * tokens : (t + 1) * tokens] = rows.T.astype(BF16)
             else:
                 value_wide[t * tokens : (t + 1) * tokens, 0:lanes] = rows.astype(BF16)
     keys_total = n * tokens
     value_wide[:, lanes:] = jnp.ones((keys_total, lanes), BF16)
 
-    def mixed_copy(source, peer):
+    rows = min(tokens, ROWS)
+    halves = range(tokens // rows)
+
+    def mixed_copy(half, source, peer):
         return remote(
-            mixed_send.at[peer],
-            mixed_got.at[source],
-            mixed_send_sem.at[peer],
-            mixed_recv_sem.at[source],
+            mixed_send.at[half, peer],
+            mixed_got.at[half, source],
+            mixed_send_sem.at[half, peer],
+            mixed_recv_sem.at[half, source],
             ctx=peer,
         )
 
-    def attend(offset, carry):
-        peer = partner(me, n - 1 - offset, n)
-        rows = min(tokens, ROWS)
-        for first in range(0, tokens, rows):
-            picked = query[peer, first : first + rows, :]
-            lane = iota((rows, lanes), 1) // head_size
+    batch = n // 2
+
+    def attend(turn, carry):
+        half = lax.rem(turn, len(halves))
+        peers = [partner(me, n - 1 - turn // len(halves) * batch - i, n) for i in range(batch)]
+        mine_rows = pl.ds(pl.multiple_of(half * rows, rows), rows)
+        lane = iota((rows, lanes), 1) // head_size
+        for peer in peers:
+            picked = query[peer, mine_rows, :]
             mixed = None
             for head in range(local_heads):
                 mine = jnp.where(lane == head, picked, jnp.zeros_like(picked))
-                scores = lax.dot_general(
-                    mine,
-                    key[...].reshape(keys_total, lanes),
-                    (((1,), (1,)), ((), ())),
-                    preferred_element_type=F32,
-                )
+                scores = jnp.dot(mine, key[...], preferred_element_type=F32)
                 weight = jnp.exp(scores - jnp.max(scores, axis=1, keepdims=True))
                 product = jnp.dot(
                     weight.astype(BF16), value_wide[...], preferred_element_type=F32
                 )
-                rows_mixed = product[:, 0:lanes] / product[:, lanes:]
-                mixed = rows_mixed if mixed is None else jnp.where(lane == head, rows_mixed, mixed)
-            mixed_send[peer, first : first + rows, :] = mixed.astype(BF16)
-
-        @pl.when(offset < n - 1)
-        def _():
-            mixed_copy(me, peer).start()
+                product = product[:, 0:lanes] / product[:, lanes:]
+                mixed = product if mixed is None else jnp.where(lane == head, product, mixed)
+            mixed_send[half, peer] = mixed.astype(BF16)
+        for i, peer in enumerate(peers):
+            if i < batch - 1:
+                mixed_copy(half, me, peer).start()
+            else:
+
+                @pl.when(turn < len(halves))
+                def _():
+                    mixed_copy(half, me, peer).start()
 
         return carry
 
-    lax.fori_loop(0, n, attend, 0)
-    mixed_got[me] = mixed_send[me]
-
-    each_peer(lambda peer: mixed_copy(peer, peer).wait_recv())
-    for piece in range(n):
-        attended[:, piece * lanes : (piece + 1) * lanes] = mixed_got[piece]
-
-    weights[0].wait()
+    lax.fori_loop(0, 2 * len(halves), attend, 0)
+    for half in halves:
+        mixed_got[half, me] = mixed_send[half, me]
+
+    hidden_width = w_fc1.shape[1]
+    tile = math.gcd(hidden_width, 512)
+    for copy in weights:
+        copy.wait()
+    for half in halves:
+        each_peer(lambda peer: mixed_copy(half, peer, peer).wait_recv())
+    attended = jnp.concatenate(
+        [
+            jnp.concatenate([mixed_got[half, piece] for piece in range(n)], axis=1)
+            for half in halves
+        ],
+        axis=0,
+    )
     stream = (
         residual[...].astype(F32)
-        + jnp.dot(attended[...], w_out[...], preferred_element_type=F32)
+        + jnp.dot(attended, w_out[...], preferred_element_type=F32)
         + out_bias[...]
     ).astype(BF16)
     stream = stream.astype(F32)
     normed[...] = norm_rows(stream, ln2_gain[...], ln2_bias[...]).astype(BF16)
     total[...] = stream + fc2_bias[...]
-
-    weights[1].wait()
-    weights[2].wait()
-    hidden_width = w_fc1.shape[1]
-    tile = math.gcd(hidden_width, 512)
     for start in range(0, hidden_width, tile):
         columns = slice(start, start + tile)
         hidden = jnp.dot(normed[...], w_fc1[:, columns], preferred_element_type=F32)
@@ -882,24 +884,27 @@
     def finish(peer):
         sum_copy(me, peer).wait_send()
         stats_copy(me, peer).wait_send()
-        mixed_copy(me, peer).wait_send()
+        part_copy(me, peer).wait_send()
+        for half in halves:
+            mixed_copy(half, me, peer).wait_send()
         relay(1, peer, replica, near).wait_send()
         relay(2, peer, replica, across).wait_send()
         relay(3, peer, across, near).wait_send()
 
     each_peer(finish)
     for step in range(pairs - 1):
-        for other in range(2):
-            part_copy(step, other).wait_send()
-        blocks_copy(step, 2 * pair_at(step) + my_side).wait_send()
-        blocks_relay(2 * pair_at(step) + my_side, pairs + step).wait_send()
-    for other in range(2):
-
-        @pl.when(my_side != other)
+        source = 2 * pair_at(step) + my_side
+        blocks_copy(step, source).wait_send()
+
+        @pl.when(source != twin_corner)
         def _():
-            part_copy(pairs - 1, other).wait_send()
+            blocks_relay(source, pairs + 1 + step).wait_send()
 
     blocks_copy(pairs - 1, twin).wait_send()
+
+    @pl.when(inside == 1)
+    def _():
+        blocks_copy(pairs, corner).wait_send()
 
 
 def shared_call(
@@ -934,7 +939,7 @@
     lanes = 128
     pairs = n // 2
     return pl.pallas_call(
-        functools.partial(shared_kernel, n, density.size * n),
+        functools.partial(shared_kernel, n, (density.shape[0] * side * side) * n),
         out_shape=jax.ShapeDtypeStruct((tokens, width), BF16),
         in_specs=[
             vmem, vmem, vmem, vmem, vmem, vmem, hbm, vmem,
@@ -943,12 +948,12 @@
         ],
         out_specs=vmem,
         scratch_shapes=[
-            pltpu.VMEM((pairs, 3, width, 2 * lanes), BF16),
+            pltpu.VMEM(w_qkv.shape, BF16),
             pltpu.VMEM(w_out.shape, BF16),
             pltpu.VMEM(w_fc1.shape, BF16),
             pltpu.VMEM(w_fc2.shape, BF16),
             *[pltpu.VMEM(table.shape, BF16) for table in tables],
-            dma((pairs, 3)),
+            dma((4,)),
             dma((3,)),
             dma((4,)),
             pltpu.VMEM((8, lanes), F32),
@@ -966,22 +971,21 @@
             pltpu.VMEM((n, tokens // 4, 3 * lanes), BF16),
             pltpu.VMEM((n, tokens, 3 * lanes), BF16),
             pltpu.VMEM((n, tokens, lanes), BF16),
-            pltpu.VMEM((n, tokens, lanes), BF16),
+            pltpu.VMEM((lanes, n * tokens), BF16),
             pltpu.VMEM((n * tokens, 2 * lanes), BF16),
-            pltpu.VMEM((n, tokens, lanes), BF16),
-            pltpu.VMEM((n, tokens, lanes), BF16),
-            pltpu.VMEM((tokens, width), BF16),
+            pltpu.VMEM((tokens // ROWS, n, ROWS, lanes), BF16),
+            pltpu.VMEM((tokens // ROWS, n, ROWS, lanes), BF16),
             pltpu.VMEM((tokens, width), F32),
             dma((n,)),
             dma((n,)),
             dma((n,)),
             dma((n,)),
-            dma((2 * pairs,)),
+            dma((2 * pairs + 1,)),
             dma((n,)),
             dma((4, n)),
             dma((4, n)),
-            dma((n,)),
-            dma((n,)),
+            dma((tokens // ROWS, n)),
+            dma((tokens // ROWS, n)),
         ],
         compiler_params=pltpu.CompilerParams(
             collective_id=1, has_side_effects=True, vmem_limit_bytes=60 * 1024 * 1024

time: 58.8 us -> 55.6 us (0.946)
  Pallas kernels: 56.7 us -> 53.6 us
    pallas_call x1, Pallas kernels: 56.7 us -> 53.6 us  [shared_call(): pl.pallas_call(functools.partial(shared_kernel, n, density.shape[0] * sid...]
where the time goes in v2:
time: 55.6 us; the launch traced here: 55.5 us
  Pallas kernels  53.6 us (96%)
  local copies, waits for them, and re-layouts  1.87 us (3%)
    pallas_call x1, Pallas kernels, shared_call(): pl.pallas_call(functools.partial(shared_kernel, n, density.shape[0] * sid...  53.6 us
    unnamed x1, local copies, waits for them, and re-layouts  1.87 us

profile of v2, /device:TPU:0, one launch (start us, length us, event | category | flops | bytes accessed | tf_op | source)
XLA Modules:
  0.0 55.5 jit_solution(13542624747357340171)
XLA Ops:
  0.0 53.6 %shard_map.190 = bf16[256,1024]{1,0:T(8,128)(2,1)} custom-call(f32[4,64,64]{2,1,0:T(8,128)} %density.1, bf16[216,1024]{1,0:T(8,128)(2,1)} %stem_weight.1, f32[1,1024]{1,0:T(1,128)} %bitcast.11, bf16[256,1024]{1,0:T(8,128)(2,1)} %pos_embed.1, f32[1,1024]{1,0:T(1,128)} %bitcast.12, f32[1,1024]{1,0:T(1,128)} %bitcast.13, bf16[1024,3072]{1,0:T(8,128)(2,1)} %w_qkv_hbm.1, ...), custom_call_target="tpu_custom_call" | custom-call | tf_op jit(solution)/shard_map/pallas_call | solution.py:941
  53.6 1.9 %copy.22 = bf16[256,1024]{1,0:T(8,128)(2,1)} copy(bf16[256,1024]{1,0:T(8,128)(2,1)} %shard_map.190) | data formatting | bytes 1048576

commit v3 on v2

--- a/solution.py
+++ b/solution.py
@@ -853,7 +853,7 @@
         mixed_got[half, me] = mixed_send[half, me]
 
     hidden_width = w_fc1.shape[1]
-    tile = math.gcd(hidden_width, 512)
+    tile = math.gcd(hidden_width, 1024)
     for copy in weights:
         copy.wait()
     for half in halves:

time: 55.6 us -> 54.9 us (0.987)
  Pallas kernels: 53.6 us -> 52.9 us
    pallas_call x1, Pallas kernels: 53.6 us -> 52.9 us  [shared_call(): pl.pallas_call(functools.partial(shared_kernel, n, density.shape[0] * sid...]
where the time goes in v3:
time: 54.9 us; the launch traced here: 54.7 us
  Pallas kernels  52.9 us (96%)
  local copies, waits for them, and re-layouts  1.87 us (3%)
    pallas_call x1, Pallas kernels, shared_call(): pl.pallas_call(functools.partial(shared_kernel, n, density.shape[0] * sid...  52.9 us
    unnamed x1, local copies, waits for them, and re-layouts  1.87 us

profile of v3, /device:TPU:0, one launch (start us, length us, event | category | flops | bytes accessed | tf_op | source)
XLA Modules:
  0.0 54.7 jit_solution(14858220585298086076)
XLA Ops:
  0.0 52.9 %shard_map.190 = bf16[256,1024]{1,0:T(8,128)(2,1)} custom-call(f32[4,64,64]{2,1,0:T(8,128)} %density.1, bf16[216,1024]{1,0:T(8,128)(2,1)} %stem_weight.1, f32[1,1024]{1,0:T(1,128)} %bitcast.11, bf16[256,1024]{1,0:T(8,128)(2,1)} %pos_embed.1, f32[1,1024]{1,0:T(1,128)} %bitcast.12, f32[1,1024]{1,0:T(1,128)} %bitcast.13, bf16[1024,3072]{1,0:T(8,128)(2,1)} %w_qkv_hbm.1, ...), custom_call_target="tpu_custom_call" | custom-call | tf_op jit(solution)/shard_map/pallas_call | solution.py:941
  52.9 1.9 %copy.22 = bf16[256,1024]{1,0:T(8,128)(2,1)} copy(bf16[256,1024]{1,0:T(8,128)(2,1)} %shard_map.190) | data formatting | bytes 1048576
